TPU v7x, 256 devices: a whole 4x4x8 slice. The times are simulated.
256 devices in a mesh: task: 8 (over y, core), param: 32 (over z, x).
Axes of the slice: x: 4, y: 4, z: 8, core: 2. Of those that a mesh axis runs over, the one named last changes fastest.
Arguments:
- params: bfloat16 [32, 2048, 4096], P('task', 'param'), may hold values from -6 to 6
- fisher: float32 [32, 2048, 4096], P('task', 'param'), may hold values from 3e-06 to 1, as said below
Outputs:
- merged: bfloat16 [2048, 4096], P('param')
Inputs may be any that keep to these rules, and one draw needn't show every extreme that they name: `fisher`: every entry is positive; scales differ strongly between tasks and between regions of rows.
All inputs are finite; a program needn't handle non-finite values.
Results may differ from a plain program's by a relative error of at most 0.00045.
Values may be sent and summed in bfloat16 or wider, within the bound.
A program may use at most 64 MiB of HBM per device.

v0:
```python
import jax
import jax.numpy as jnp
from jax import lax
from jax.sharding import PartitionSpec as P


def sent_to_all(array, axis):
    peers = lax.axis_size(axis)
    return lax.all_to_all(
        jnp.broadcast_to(array[None], (peers, *array.shape)), axis, 0, 0, tiled=True
    )


def gathered_once(array, axis):
    leaves = jax.tree.leaves(array)
    turns = sorted(range(len(leaves)), key=lambda k: -leaves[k].size)
    width = (1, *leaves[turns[0]].shape)[-1]
    lines = [
        jnp.pad(leaves[k].reshape(-1), (0, -leaves[k].size % width)).reshape(-1, width)
        for k in turns
    ]
    both, at, found = (sent_to_all(jnp.concatenate(lines), axis), 0, {})
    for k, line in zip(turns, lines):
        share = both[:, at : at + len(line)].reshape(len(both), -1)
        found[k] = share[:, : leaves[k].size].reshape(-1, *leaves[k].shape)
        at += len(line)
    numbers = iter(range(len(leaves)))
    return jax.tree.map(lambda _: found[next(numbers)], array)


def folded_in_pairs(pieces, combine):
    while len(jax.tree.leaves(pieces)[0]) > 1:
        pieces = jax.vmap(combine)(
            *(jax.tree.map(lambda part: part[side::2], pieces) for side in (0, 1))
        )
    return jax.tree.map(lambda part: part[0], pieces)


def merged(array, axis, combine):
    pieces = gathered_once(array, axis)
    return folded_in_pairs(pieces, combine)


def cut_along(array, dim, peers):
    before, after = (array.shape[:dim], array.shape[dim + 1 :])
    return jnp.moveaxis(array.reshape(*before, peers, -1, *after), dim, 0)


def sent_and_summed(array, axis, dim):
    peers = lax.axis_size(axis)
    pieces = lax.all_to_all(cut_along(array, dim, peers), axis, 0, 0, tiled=True)
    return jnp.sum(pieces, axis=0)


def in_order(pieces, dim):
    shape = list(pieces.shape[1:])
    shape[dim] *= pieces.shape[0]
    return jnp.moveaxis(pieces, 0, dim).reshape(shape)


def collect(array, axis, dim):
    pieces = sent_to_all(array, axis)
    return in_order(pieces, dim)


def joined(first, second):
    return (jnp.maximum(first[0], second[0]), first[1] + second[1])


def local(params, fisher):
    local_peak = jnp.max(fisher, axis=(1, 2))
    local_total = jnp.sum(fisher, axis=(1, 2))
    peak, total = merged((local_peak, local_total), "param", joined)
    count = float(fisher.shape[1] * lax.axis_size("param") * fisher.shape[2])
    factor = count * peak / total
    weight = jnp.clip(fisher / peak[:, None, None], 0.002, 0.25) * factor[:, None, None]
    numer = jnp.sum(weight * params.astype(jnp.float32), axis=0)
    denom = jnp.sum(weight, axis=0)
    share_numer, share_denom = (
        sent_and_summed(numer, "task", 0),
        sent_and_summed(denom, "task", 0),
    )
    portion = (share_numer / share_denom).astype(jnp.bfloat16)
    return collect(portion, "task", 0)


def solution(mesh):
    in_specs = (P("task", "param", None), P("task", "param", None))
    out_specs = P("param", None)
    return jax.shard_map(local, mesh=mesh, in_specs=in_specs, out_specs=out_specs, check_vma=False)
```

profile of v0, /device:TPU:1, one launch (start us, length us, event | category | flops | bytes accessed | tf_op | source)
XLA Modules:
  0.0 84.3 jit_solution(7418499841446395806)
XLA Ops:
  0.0 0.0 copy-start
  0.0 2.7 %fusion.1 = (f32[4]{0:T(128)S(1)}, f32[4]{0:T(128)S(1)}) fusion(f32[4,64,4096]{2,1,0:T(8,128)} %param.3), kind=kLoop, calls=%fused_computation.8 | loop fusion | flops 2097144 | bytes 4194336 | tf_op jit(solution)/shard_map/reduce_max | solution.py:71
  2.8 20.4 %all_to_all.20 = f32[32,2,4]{2,1,0:T(2,128)S(1)} all-to-all(f32[32,2,4]{2,1,0:T(2,128)S(1)} %broadcast_in_dim.4), channel_id=1, replica_groups=mesh['task'=8,'param'=32] {'param'}, dimensions={0} | all-to-all | bytes 2048 | tf_op jit(solution)/shard_map/all_to_all | solution.py:9
  23.2 0.1 copy.5
  23.2 0.1 slice.72
  23.3 0.1 slice.71
  23.5 0.1 slice.74
  23.6 0.1 slice.73
  23.7 0.1 slice.76
  23.8 0.1 slice.75
  23.9 0.1 slice.78
  24.0 0.1 slice.77
  24.1 0.1 copy.6
  24.1 0.1 slice.83
  24.3 0.1 slice.82
  24.4 0.1 slice.85
  24.5 0.1 slice.84
  24.6 0.1 slice.87
  24.7 0.1 slice.86
  24.8 0.1 slice.89
  24.9 0.1 slice.88
  25.0 0.2 add_reduce_fusion
  25.2 0.0 copy-done
  25.2 4.6 %fusion = (f32[64,4096]{1,0:T(8,128)}, f32[64,4096]{1,0:T(8,128)S(1)}) fusion(f32[4]{0:T(128)S(1)} %multiply_divide_fusion, f32[4,64,4096]{2,1,0:T(8,128)} %param.3, f32[4]{0:T(128)S(1)} %get-tuple-element.12, bf16[4,64,4096]{2,1,0:T(8,128)(2,1)S(1)} %copy-done), kind=kLoop, calls=%fused_computation.7 | loop fusion | flops 6815744 | bytes 8388640 | tf_op jit(solution)/shard_map/reduce_sum | solution.py:78
  29.9 21.3 %all_to_all.21 = f32[8,8,4096]{2,1,0:T(8,128)S(1)} all-to-all(f32[8,8,4096]{2,1,0:T(8,128)S(1)} %bitcast.7), channel_id=1, replica_groups=mesh['task'=8,'param'=32] {'task'}, dimensions={0} | all-to-all | bytes 2097152 | tf_op jit(solution)/shard_map/all_to_all | solution.py:51
  51.2 4.5 %all-to-all-start.2 = ((f32[8,8,4096]{2,1,0:T(8,128)}), f32[8,8,4096]{2,1,0:T(8,128)S(1)}, u32[]{:S(2)}, u32[]{:S(2)}) async-start(f32[8,8,4096]{2,1,0:T(8,128)} %bitcast.5), calls=%async_computation.2 | async-start | bytes 2097152 | tf_op jit(solution)/shard_map/all_to_all | solution.py:51
  55.7 0.1 reduce_sum.47
  55.7 14.9 %all-to-all-done.2 = f32[8,8,4096]{2,1,0:T(8,128)S(1)} async-done(((f32[8,8,4096]{2,1,0:T(8,128)}), f32[8,8,4096]{2,1,0:T(8,128)S(1)}, u32[]{:S(2)}, u32[]{:S(2)}) %all-to-all-start.2) | async-done | bytes 1048608 | tf_op jit(solution)/shard_map/all_to_all | solution.py:51
  70.7 0.1 reduce_sum.49
  70.8 12.7 %all_to_all.22 = bf16[8,8,4096]{2,1,0:T(8,128)(2,1)S(1)} all-to-all(bf16[8,8,4096]{2,1,0:T(8,128)(2,1)S(1)} %broadcast_in_dim.5), channel_id=1, replica_groups=mesh['task'=8,'param'=32] {'task'}, dimensions={0} | all-to-all | bytes 1048576 | tf_op jit(solution)/shard_map/all_to_all | solution.py:9
  83.5 0.8 copy.8
  (14 shorter events, 0.2 us)
Async XLA Ops:
  0.0 25.2 %copy-start = (bf16[4,64,4096]{2,1,0:T(8,128)(2,1)S(1)}, bf16[4,64,4096]{2,1,0:T(8,128)(2,1)}, u32[]{:S(2)}) copy-start(bf16[4,64,4096]{2,1,0:T(8,128)(2,1)} %param.2) | copy-start | bytes 6291460
  51.2 19.5 %all-to-all-start.2 = ((f32[8,8,4096]{2,1,0:T(8,128)}), f32[8,8,4096]{2,1,0:T(8,128)S(1)}, u32[]{:S(2)}, u32[]{:S(2)}) async-start(f32[8,8,4096]{2,1,0:T(8,128)} %bitcast.5), calls=%async_computation.2 | async-start | bytes 2097152 | tf_op jit(solution)/shard_map/all_to_all | solution.py:51
where the time goes:
time: 84.6 us; the launch traced here: 84.3 us
  blocking collectives  54.3 us (64%)
  waiting for transfers between devices  14.9 us (18%)
  other arithmetic  7.82 us (9%)
  starting transfers between devices  4.5 us (5%)
  local copies, waits for them, and re-layouts  2.61 us (3%)
    all_to_all x2, blocking collectives, sent_to_all(): lax.all_to_all(jnp.broadcast_to(array[None], (peers, *array.shape)), axis...  33 us
    all_to_all x1, blocking collectives, sent_and_summed(): lax.all_to_all(cut_along(array, dim, peers), axis, 0, 0, tiled=True)  21.3 us
    all_to_all x1, waiting for transfers between devices, sent_and_summed(): lax.all_to_all(cut_along(array, dim, peers), axis, 0, 0, tiled=True)  14.9 us
    reduce_sum x1, other arithmetic, local(): denom = jnp.sum(weight, axis=0)  4.64 us
    all_to_all x1, starting transfers between devices, sent_and_summed(): lax.all_to_all(cut_along(array, dim, peers), axis, 0, 0, tiled=True)  4.5 us
    reduce_max x1, other arithmetic, local(): local_peak = jnp.max(fisher, axis=(1, 2))  2.75 us
  transfers between devices with their start and end apart: 1, of which 1 were waited for; matrix products, arithmetic and copies ran while one was open for 0% of the time, Pallas kernels for 0%

commit v1 on v0

v1 whole, which is shorter than its diff:
```python
import functools

import jax
import jax.numpy as jnp
from jax import lax
from jax.experimental import pallas as pl
from jax.experimental.pallas import tpu as pltpu
from jax.sharding import PartitionSpec as P

F32, BF16 = jnp.float32, jnp.bfloat16
MESH = pl.DeviceIdType.MESH
X, Y, Z, CORES = 4, 4, 8, 2
TASKS, ROWS, COLS = 4, 64, 4096
HALF = ROWS // CORES
CHUNK = COLS // Y
PIECES = 4
WIDE = CHUNK // PIECES
COUNT = float(ROWS * X * Z * COLS)
LEAST, MOST = 0.002, 0.25


def remote(src, dst, send, recv, where):
    return pltpu.make_async_remote_copy(
        src_ref=src, dst_ref=dst, send_sem=send, recv_sem=recv, device_id=where, device_id_type=MESH
    )


def kernel(
    params, fisher, out, fi, fo, pa, near, far, sa, sc, sb, so, ra, rc, rb,
    load_f, load_p, swap_f, swap_p, near_s, near_r, far_s, far_r,
    a_s, a_r, b_s, b_r, c_s, c_r, ag_s, ag_r, fw_s, fw_r,
):
    task, place = lax.axis_index("task"), lax.axis_index("param")
    core, y = lax.rem(task, CORES), lax.div(task, CORES)
    x, z = lax.rem(place, X), lax.div(place, X)
    other = 1 - core

    def at_xc(dx, dc):
        c = core if dc == 0 else other
        return (y * CORES + c, z * X + lax.rem(x + dx, X))

    def at_z(dz):
        return (task, lax.rem(z + dz, Z) * X + x)

    def at_y(dy):
        return (lax.rem(y + dy, Y) * CORES + core, place)

    partner = (y * CORES + other, place)
    nears = [(dx, dc) for dx in range(X) for dc in range(CORES) if dx or dc]

    barrier = pltpu.get_barrier_semaphore()
    peers = [at_z(dz) for dz in (4, 3, 5, 2, 6, 1, 7)] + [at_xc(*n) for n in nears] + [at_y(dy) for dy in (2, 1, 3)]
    for peer in peers:
        pl.semaphore_signal(barrier, inc=1, device_id=peer, device_id_type=MESH)

    mine = pl.ds(pl.multiple_of(core * HALF, HALF), HALF)
    yours = pl.ds(pl.multiple_of(other * HALF, HALF), HALF)
    loads = []
    for t in range(TASKS):
        for half, (rows, dst) in enumerate(((yours, fo.at[t]), (mine, fi.at[t]))):
            copy = pltpu.make_async_copy(fisher.at[t, rows, :], dst, load_f.at[t, half])
            copy.start()
            loads.append(copy)
    loads_p = []
    for t in range(TASKS):
        copy = pltpu.make_async_copy(params.at[t, mine, :], pa.at[t], load_p.at[t])
        copy.start()
        loads_p.append(copy)

    lane = lax.broadcasted_iota(jnp.int32, (1, 128), 1)
    row = jnp.zeros((1, 128), F32)

    def stats(ref, t, carry):
        def step(k, c):
            v = ref[t, :, pl.ds(pl.multiple_of(k * 128, 128), 128)]
            return jnp.maximum(c[0], v), c[1] + v

        return lax.fori_loop(0, COLS // 128, step, carry, unroll=8)

    for t in range(TASKS):
        carry = (jnp.zeros((HALF, 128), F32), jnp.zeros((HALF, 128), F32))
        loads[2 * t].wait()
        carry = stats(fo, t, carry)
        loads[2 * t + 1].wait()
        top, tot = stats(fi, t, carry)
        top = jnp.max(jnp.max(top, axis=0, keepdims=True), axis=1, keepdims=True)
        tot = jnp.sum(jnp.sum(tot, axis=0, keepdims=True), axis=1, keepdims=True)
        row = jnp.where(lane == core * TASKS + t, top, row)
        row = jnp.where(lane == 8 + core * TASKS + t, tot, row)
    near[0] = row

    pl.semaphore_wait(barrier, len(peers))

    near_copies = []
    for i, (dx, dc) in enumerate(nears):
        slot = dx * CORES + dc
        copy = remote(near.at[0], near.at[slot], near_s.at[slot], near_r.at[slot], at_xc(dx, dc))
        copy.start()
        near_copies.append(copy)
    swaps = []
    for t in range(TASKS):
        copy = remote(fo.at[t], fi.at[TASKS + t], swap_f.at[0, t], swap_f.at[1, t], partner)
        copy.start()
        swaps.append(copy)
    for t in range(TASKS):
        copy = remote(params.at[t, yours, :], pa.at[TASKS + t], swap_p.at[0, t], swap_p.at[1, t], partner)
        copy.start()
        swaps.append(copy)

    def combined(ref, n):
        top, tot = ref[0], ref[0]
        for i in range(1, n):
            top, tot = jnp.maximum(top, ref[i]), tot + ref[i]
        return jnp.where(lane < 8, top, tot)

    for copy in near_copies:
        copy.wait_recv()
    far[0] = combined(near, X * CORES)
    far_copies = []
    for dz in (4, 3, 5, 2, 6, 1, 7):
        copy = remote(far.at[0], far.at[dz], far_s.at[dz], far_r.at[dz], at_z(dz))
        copy.start()
        far_copies.append(copy)
    for copy in loads_p:
        copy.wait()
    for copy in swaps:
        copy.wait_recv()
    for copy in far_copies:
        copy.wait_recv()
    row = combined(far, Z)
    scale_row = COUNT / row
    scale, low, high = [], [], []
    for t in range(2 * TASKS):
        at = (core if t < TASKS else other) * TASKS + t % TASKS
        top = jnp.sum(jnp.where(lane == at, row, 0.0))
        s = jnp.sum(jnp.where(lane == 8 + at, scale_row, 0.0))
        scale.append(s)
        low.append(LEAST * top * s)
        high.append(MOST * top * s)

    def partial(chunk, p, dst):
        cols = pl.ds(pl.multiple_of(chunk * CHUNK + p * WIDE, WIDE), WIDE)
        numer = denom = jnp.zeros((HALF, WIDE), F32)
        for t in range(2 * TASKS):
            w = jnp.minimum(jnp.maximum(fi[t, :, cols] * scale[t], low[t]), high[t])
            denom = denom + w
            numer = numer + w * pa[t, :, cols].astype(F32)
        dst[p, 0] = numer
        dst[p, 1] = denom

    step = 2 * core - 1
    ahead, behind, across = lax.rem(y + step + Y, Y), lax.rem(y - step + Y, Y), lax.rem(y + 2, Y)
    to_ahead, to_behind = (ahead * CORES + core, place), (behind * CORES + core, place)
    copies_a, copies_b, copies_c = [], [], []
    for p in range(PIECES):
        partial(across, p, sa)
        copies_a.append(remote(sa.at[p], ra.at[p], a_s.at[p], a_r.at[p], to_ahead))
        copies_a[p].start()
        partial(behind, p, sc)
        copies_c.append(remote(sc.at[p], rc.at[p], c_s.at[p], c_r.at[p], to_behind))
        copies_c[p].start()
    for p in range(PIECES):
        partial(ahead, p, sb)
    for p in range(PIECES):
        partial(y, p, so)
    for p in range(PIECES):
        copies_a[p].wait_recv()
        sb[p] = sb[p] + ra[p]
        copies_b.append(remote(sb.at[p], rb.at[p], b_s.at[p], b_r.at[p], to_ahead))
        copies_b[p].start()

    def block(chunk, p):
        return out.at[mine, pl.ds(pl.multiple_of(chunk * CHUNK + p * WIDE, WIDE), WIDE)]

    gathers, forwards = {}, {}

    def finish(p):
        copies_c[p].wait_recv()
        copies_b[p].wait_recv()
        total = so[p] + rc[p] + rb[p]
        here = block(y, p)
        here[...] = (total[0] / total[1]).astype(BF16)
        for dy in (2, 1, 3):
            gathers[p, dy] = remote(here, here, ag_s.at[p, dy], ag_r.at[p, dy], at_y(dy))
            gathers[p, dy].start()
        forwards[p, 0] = remote(here, here, fw_s.at[p, 0], fw_r.at[p, 0], partner)
        forwards[p, 0].start()

    def forward(p):
        for dy in (1, 3, 2):
            gathers[p, dy].wait_recv()
            there = block(lax.rem(y - dy + Y, Y), p)
            forwards[p, dy] = remote(there, there, fw_s.at[p, dy], fw_r.at[p, dy], partner)
            forwards[p, dy].start()

    for p in range(PIECES):
        finish(p)
        if p >= 2:
            forward(p - 2)
    forward(PIECES - 2)
    forward(PIECES - 1)

    for copy in near_copies + far_copies + swaps + copies_a + copies_b + copies_c + list(gathers.values()):
        copy.wait_send()
    for copy in forwards.values():
        copy.wait()


def local(params, fisher):
    dma = pltpu.SemaphoreType.DMA
    pieces = pltpu.VMEM((PIECES, 2, HALF, WIDE), F32)
    return pl.pallas_call(
        kernel,
        out_shape=jax.ShapeDtypeStruct((ROWS, COLS), BF16),
        in_specs=[pl.BlockSpec(memory_space=pl.ANY)] * 2,
        out_specs=pl.BlockSpec(memory_space=pltpu.VMEM),
        scratch_shapes=[
            pltpu.VMEM((2 * TASKS, HALF, COLS), F32),
            pltpu.VMEM((TASKS, HALF, COLS), F32),
            pltpu.VMEM((2 * TASKS, HALF, COLS), BF16),
            pltpu.VMEM((X * CORES, 1, 128), F32),
            pltpu.VMEM((Z, 1, 128), F32),
            *[pieces] * 7,
            dma((TASKS, 2)), dma((TASKS,)), dma((2, TASKS)), dma((2, TASKS)),
            *[dma((8,))] * 4,
            *[dma((PIECES,))] * 6,
            *[dma((PIECES, Y))] * 4,
        ],
        compiler_params=pltpu.CompilerParams(collective_id=0, has_side_effects=True),
        name="merge",
    )(params, fisher)


def solution(mesh):
    in_specs = (P("task", "param", None), P("task", "param", None))
    return jax.shard_map(local, mesh=mesh, in_specs=in_specs, out_specs=P("param", None), check_vma=False)
```

time: 84.6 us -> 38.9 us (0.46)
  blocking collectives: 54.3 us -> 0 us
  Pallas kernels: 0 us -> 36.9 us
  waiting for transfers between devices: 14.9 us -> 0 us
  other arithmetic: 7.82 us -> 0 us
  starting transfers between devices: 4.5 us -> 0 us
    all_to_all x3 -> x0, blocking collectives: 54.3 us -> none  [the longest x2 33 us: sent_to_all(): lax.all_to_all(jnp.broadcast_to(array[None], (peers, *array.shape)), axis...]
    pallas_call x0 -> x1, Pallas kernels: none -> 36.9 us  [local(): pl.pallas_call(kernel, out_shape=jax.ShapeDtypeStruct((ROWS, COLS), BF16)...]
    all_to_all x1 -> x0, waiting for transfers between devices: 14.9 us -> none  [sent_and_summed(): lax.all_to_all(cut_along(array, dim, peers), axis, 0, 0, tiled=True)]
    reduce_sum x3 -> x0, other arithmetic: 4.75 us -> none  [the longest x1 4.64 us: local(): denom = jnp.sum(weight, axis=0)]
    all_to_all x1 -> x0, starting transfers between devices: 4.5 us -> none  [sent_and_summed(): lax.all_to_all(cut_along(array, dim, peers), axis, 0, 0, tiled=True)]
    reduce_max x1 -> x0, other arithmetic: 2.75 us -> none  [local(): local_peak = jnp.max(fisher, axis=(1, 2))]
    slice x19 -> x0, local copies, waits for them, and re-layouts: 1.77 us -> none  [the longest x16 1.59 us: folded_in_pairs(): part[side::2]]
    unnamed x3 -> x1, local copies, waits for them, and re-layouts: 0.8 us -> 1.87 us
  transfers between devices with their start and end apart: 1 -> 0, of which waited for: 1 -> 0; matrix products, arithmetic and copies ran while one was open for 0% -> 0% of each run, Pallas kernels for 0% -> 0%
where the time goes in v1:
time: 38.9 us; the launch traced here: 38.8 us
  Pallas kernels  36.9 us (95%)
  local copies, waits for them, and re-layouts  1.87 us (5%)
    pallas_call x1, Pallas kernels, local(): pl.pallas_call(kernel, out_shape=jax.ShapeDtypeStruct((ROWS, COLS), BF16)...  36.9 us
    unnamed x1, local copies, waits for them, and re-layouts  1.87 us

profile of v1, /device:TPU:1, one launch (start us, length us, event | category | flops | bytes accessed | tf_op | source)
XLA Modules:
  0.0 38.8 jit_solution(9333868904869011374)
XLA Ops:
  0.0 36.9 %merge.1 = bf16[64,4096]{1,0:T(8,128)(2,1)} custom-call(bf16[4,64,4096]{2,1,0:T(8,128)(2,1)} %params.1, f32[4,64,4096]{2,1,0:T(8,128)} %fisher.1), custom_call_target="tpu_custom_call" | custom-call | tf_op jit(solution)/shard_map/merge/pallas_call | solution.py:212
  37.0 1.9 %copy.4 = bf16[64,4096]{1,0:T(8,128)(2,1)} copy(bf16[64,4096]{1,0:T(8,128)(2,1)} %merge.1) | data formatting | bytes 1048576

commit v2 on v1

--- a/solution.py
+++ b/solution.py
@@ -211,7 +211,7 @@
     pieces = pltpu.VMEM((PIECES, 2, HALF, WIDE), F32)
     return pl.pallas_call(
         kernel,
-        out_shape=jax.ShapeDtypeStruct((ROWS, COLS), BF16),
+        out_shape=pltpu.VMEM((ROWS, COLS), BF16),
         in_specs=[pl.BlockSpec(memory_space=pl.ANY)] * 2,
         out_specs=pl.BlockSpec(memory_space=pltpu.VMEM),
         scratch_shapes=[

time: 38.9 us -> 37 us (0.951)
  local copies, waits for them, and re-layouts: 1.87 us -> 0.8 us
  Pallas kernels: 36.9 us -> 36.2 us
    unnamed x1, local copies, waits for them, and re-layouts: 1.87 us -> 0.8 us
    pallas_call x1, Pallas kernels: 36.9 us -> 36.2 us  [local(): pl.pallas_call(kernel, out_shape=pltpu.VMEM((ROWS, COLS), BF16), in_specs...]
where the time goes in v2:
time: 37 us
  Pallas kernels  36.2 us (98%)
  local copies, waits for them, and re-layouts  0.8 us (2%)
    pallas_call x1, Pallas kernels, local(): pl.pallas_call(kernel, out_shape=pltpu.VMEM((ROWS, COLS), BF16), in_specs...  36.2 us
    unnamed x1, local copies, waits for them, and re-layouts  0.8 us

profile of v2, /device:TPU:1, one launch (start us, length us, event | category | flops | bytes accessed | tf_op | source)
XLA Modules:
  0.0 37.0 jit_solution(6055102539863190094)
XLA Ops:
  0.0 36.2 %merge.1 = bf16[64,4096]{1,0:T(8,128)(2,1)S(1)} custom-call(bf16[4,64,4096]{2,1,0:T(8,128)(2,1)} %params.1, f32[4,64,4096]{2,1,0:T(8,128)} %fisher.1), custom_call_target="tpu_custom_call" | custom-call | tf_op jit(solution)/shard_map/merge/pallas_call | solution.py:212
  36.2 0.8 %copy.4 = bf16[64,4096]{1,0:T(8,128)(2,1)} copy(bf16[64,4096]{1,0:T(8,128)(2,1)S(1)} %merge.1) | data formatting | bytes 1048576
